TPU v7x, 32 devices: a whole 2x2x4 slice. The times are simulated.
32 devices in a mesh: grp: 2 (over x), rep: 8 (over z, y), blk: 2 (over core).
Axes of the slice: x: 2, y: 2, z: 4, core: 2. Of those that a mesh axis runs over, the one named last changes fastest.
Arguments:
- factors: float32 [16, 1280, 1280], P('grp', ('blk', 'rep')), as said below
- damping: float32 [16], P('grp'), may hold values from 0.1 to 1
Outputs:
- root: float32 [16, 1280, 1280], P('grp', ('blk', 'rep'))
- inv_root: float32 [16, 1280, 1280], P('grp', ('blk', 'rep'))
Inputs may be any that keep to these rules, and one draw needn't show every extreme that they name: `factors`: every factor is symmetric positive semidefinite.
All inputs are finite; a program needn't handle non-finite values.
Results may differ from a plain program's by a relative error of at most 0.0035.
The roundings to bfloat16 on the way count: a program that leaves them out, or rounds other values in their place, can miss the bound.
Values may be sent and summed in bfloat16 or wider, within the bound.
No kernel may reach another device: no remote copies, remote signals or barrier semaphores. Data moves between devices by JAX's collectives and lax.ppermute only.
A program may use at most 128 MiB of HBM per device.

v0:
```python
import jax
import jax.numpy as jnp
from jax import lax
from jax.sharding import PartitionSpec as P

ITERS = 4


def per_device(factors, damping):
    fac_grp = factors.shape[0]
    row_count = factors.shape[1]
    order_full = factors.shape[2]
    rep_count = lax.axis_size("rep")
    fac_rep = fac_grp // rep_count
    blk_rows = row_count * rep_count
    blk_idx = lax.axis_index("blk")
    rep_idx = lax.axis_index("rep")
    row_ids = blk_idx * blk_rows + rep_idx * row_count + lax.iota(jnp.int32, row_count)
    col_ids = lax.iota(jnp.int32, order_full)
    eye_block = (row_ids[:, None] == col_ids[None, :]).astype(jnp.float32)
    damped = factors + damping[:, None, None] * eye_block[None, :, :]
    factor_norms = jnp.sqrt(lax.psum(jnp.sum(damped * damped, axis=(1, 2)), ("rep", "blk")))
    own_rows = lax.all_to_all(damped, "rep", split_axis=0, concat_axis=1, tiled=True)
    own_norms = lax.dynamic_slice_in_dim(factor_norms, rep_idx * fac_rep, fac_rep)
    iterate = (own_rows / own_norms[:, None, None]).astype(jnp.bfloat16)
    iter_rows = blk_idx * blk_rows + lax.iota(jnp.int32, blk_rows)
    eye_rows = (iter_rows[:, None] == col_ids[None, :]).astype(jnp.float32)
    inverse = eye_rows[None, :, :].astype(jnp.bfloat16)
    for sweep_idx in range(ITERS):
        whole_iter, whole_inv = (
            lax.all_gather(iterate, "blk", axis=1, tiled=True),
            lax.all_gather(inverse, "blk", axis=1, tiled=True),
        )
        eye_full = jnp.eye(order_full, dtype=jnp.float32)
        moment_full = jnp.einsum(
            "fik,fkj->fij", whole_inv, whole_iter, preferred_element_type=jnp.float32
        )
        step_full = ((3.0 * eye_full[None, :, :] - moment_full) * 0.5).astype(jnp.bfloat16)
        step_rows = lax.dynamic_slice_in_dim(step_full, blk_idx * blk_rows, blk_rows, 1)
        new_iterate = jnp.einsum(
            "fik,fkj->fij", iterate, step_full, preferred_element_type=jnp.float32
        )
        new_inverse = jnp.einsum(
            "fik,fkj->fij", step_rows, whole_inv, preferred_element_type=jnp.float32
        )
        iterate = new_iterate.astype(jnp.bfloat16)
        inverse = new_inverse.astype(jnp.bfloat16)
    root_block, inv_block = (
        lax.all_to_all(iterate, "rep", split_axis=1, concat_axis=0, tiled=True),
        lax.all_to_all(inverse, "rep", split_axis=1, concat_axis=0, tiled=True),
    )
    root_scale = jnp.sqrt(factor_norms)[:, None, None]
    return (root_block.astype(jnp.float32) * root_scale, inv_block.astype(jnp.float32) / root_scale)


def solution(mesh):
    return jax.shard_map(
        per_device,
        mesh=mesh,
        in_specs=(P("grp", ("blk", "rep"), None), P("grp")),
        out_specs=(P("grp", ("blk", "rep"), None), P("grp", ("blk", "rep"), None)),
        check_vma=False,
    )
```

profile of v0, /device:TPU:0, one launch (start us, length us, event | category | flops | bytes accessed | tf_op | source)
XLA Modules:
  0.0 384.2 jit_solution(16059342983351797581)
XLA Ops:
  7.2 0.1 fusion.21
  7.3 4.3 %multiply_reduce_fusion = (f32[8]{0:T(128)S(1)}, f32[8,80,1280]{2,1,0:T(8,128)}) fusion(f32[8,80,1280]{2,1,0:T(8,128)} %param.2, f32[80,1280]{1,0:T(8,128)S(1)} %fusion.21, f32[8]{0:T(128)} %param.3), kind=kLoop, calls=%fused_computation.20 | loop fusion | flops 3276792 | bytes 6963264 | tf_op jit(solution)/shard_map/reduce_sum | solution.py:22
  11.6 7.3 %all-to-all-start = ((f32[8,80,1280]{2,1,0:T(8,128)}), f32[8,80,1280]{2,1,0:T(8,128)S(1)}, u32[]{:S(2)}, u32[]{:S(2)}) async-start(f32[8,80,1280]{2,1,0:T(8,128)} %get-tuple-element.3), calls=%async_computation | async-start | bytes 6553600 | tf_op jit(solution)/shard_map/all_to_all | solution.py:23
  19.0 1.5 convert_convert_fusion
  20.5 80.0 %psum.7 = f32[8]{0:T(128)S(1)} all-reduce(f32[8]{0:T(128)S(1)} %get-tuple-element.2), channel_id=1, replica_groups=mesh['grp'=2,'rep'=8,'blk'=2] {'rep','blk'}, use_global_device_ids=true, to_apply=%region_1.0 | all-reduce | flops 8 | bytes 64 | tf_op jit(solution)/shard_map/psum | solution.py:22
  100.6 0.6 dynamic_slice.2
  101.2 2.0 divide_convert_fusion
  103.3 20.4 %all-gather.17.cloned.1.call-done = bf16[1,1280,1280]{2,1,0:T(8,128)(2,1)} async-done(((bf16[1,640,1280]{2,1,0:T(8,128)(2,1)}), bf16[1,1280,1280]{2,1,0:T(8,128)(2,1)}) %all-gather.17.cloned.1.call-update) | async-done | bytes 3276816 | tf_op jit(solution)/shard_map/all_gather | solution.py:31
  123.7 7.3 %fusion.4 = bf16[1280,1280]{1,0:T(8,128)(2,1)S(1)} fusion(bf16[1,1280,1280]{2,1,0:T(8,128)(2,1)} %all-gather.17.cloned.1.call-done, bf16[1,1280,1280]{2,1,0:T(8,128)(2,1)} %all-gather.15.cloned.1.call-done), kind=kOutput, calls=%fused_computation.8 | convolution fusion | flops 4202496000 | bytes 9830400 | tf_op jit(solution)/shard_map/fik,fkj->fij/dot_general | solution.py:35
  131.1 1.7 copy-done.5
  132.8 3.5 convolution_convert_fusion.6
  136.3 0.0 all-gather.19.cloned.1.call-start
  136.4 5.9 %fusion.12 = bf16[640,1280]{1,0:T(8,128)(2,1)} fusion(bf16[1,1280,1280]{2,1,0:T(8,128)(2,1)} %all-gather.15.cloned.1.call-done, bf16[1280,1280]{1,0:T(8,128)(2,1)} %copy-done.5, s32[]{:T(128)S(6)} %select_n.10), kind=kOutput, calls=%fused_computation.22 | convolution fusion | flops 2097971200 | bytes 6553604 | tf_op jit(solution)/shard_map/fik,fkj->fij/dot_general | solution.py:43
  142.3 0.2 all-gather.25.cloned.1.call-start
  142.5 7.5 %all-gather.21.cloned.1.call-done = bf16[1280,1280]{1,0:T(8,128)(2,1)} async-done(((bf16[640,1280]{1,0:T(8,128)(2,1)}), bf16[1280,1280]{1,0:T(8,128)(2,1)}) %all-gather.21.cloned.1.call-update) | async-done | bytes 3276816 | tf_op jit(solution)/shard_map/all_gather | solution.py:31
  150.0 15.5 %all-gather.19.cloned.1.call-done = bf16[1280,1280]{1,0:T(8,128)(2,1)} async-done(((bf16[640,1280]{1,0:T(8,128)(2,1)}), bf16[1280,1280]{1,0:T(8,128)(2,1)}) %all-gather.19.cloned.1.call-update) | async-done | bytes 3276816 | tf_op jit(solution)/shard_map/all_gather | solution.py:32
  165.5 7.3 %fusion.5 = bf16[1280,1280]{1,0:T(8,128)(2,1)S(1)} fusion(bf16[1280,1280]{1,0:T(8,128)(2,1)} %all-gather.19.cloned.1.call-done, bf16[1280,1280]{1,0:T(8,128)(2,1)} %all-gather.21.cloned.1.call-done), kind=kOutput, calls=%fused_computation.9 | convolution fusion | flops 4202496000 | bytes 9830400 | tf_op jit(solution)/shard_map/fik,fkj->fij/dot_general | solution.py:35
  172.8 1.7 copy-done.7
  174.5 3.5 convolution_convert_fusion.5
  178.1 5.9 %convolution_convert_fusion.4 = bf16[640,1280]{1,0:T(8,128)(2,1)} fusion(bf16[1280,1280]{1,0:T(8,128)(2,1)} %all-gather.19.cloned.1.call-done, bf16[1280,1280]{1,0:T(8,128)(2,1)} %copy-done.7, s32[]{:T(128)S(6)} %select_n.10), kind=kOutput, calls=%fused_computation.27 | convolution fusion | flops 2097971200 | bytes 6553604 | tf_op jit(solution)/shard_map/fik,fkj->fij/dot_general | solution.py:43
  184.1 7.6 %all-gather.25.cloned.1.call-done = bf16[1280,1280]{1,0:T(8,128)(2,1)} async-done(((bf16[640,1280]{1,0:T(8,128)(2,1)}), bf16[1280,1280]{1,0:T(8,128)(2,1)}) %all-gather.25.cloned.1.call-update) | async-done | bytes 3276816 | tf_op jit(solution)/shard_map/all_gather | solution.py:31
  191.7 15.5 %all-gather.23.cloned.1.call-done = bf16[1280,1280]{1,0:T(8,128)(2,1)} async-done(((bf16[640,1280]{1,0:T(8,128)(2,1)}), bf16[1280,1280]{1,0:T(8,128)(2,1)}) %all-gather.23.cloned.1.call-update) | async-done | bytes 3276816 | tf_op jit(solution)/shard_map/all_gather | solution.py:32
  207.2 7.3 %fusion.6 = bf16[1280,1280]{1,0:T(8,128)(2,1)S(1)} fusion(bf16[1280,1280]{1,0:T(8,128)(2,1)} %all-gather.23.cloned.1.call-done, bf16[1280,1280]{1,0:T(8,128)(2,1)} %all-gather.25.cloned.1.call-done), kind=kOutput, calls=%fused_computation.10 | convolution fusion | flops 4202496000 | bytes 9830400 | tf_op jit(solution)/shard_map/fik,fkj->fij/dot_general | solution.py:35
  214.6 1.7 copy-done.8
  216.3 3.5 convolution_convert_fusion.3
  219.8 0.3 all-gather.27.cloned.1.call-start
  220.1 5.9 %convolution_convert_fusion.2 = bf16[640,1280]{1,0:T(8,128)(2,1)} fusion(bf16[1280,1280]{1,0:T(8,128)(2,1)} %all-gather.23.cloned.1.call-done, bf16[1280,1280]{1,0:T(8,128)(2,1)} %copy-done.8, s32[]{:T(128)S(6)} %select_n.10), kind=kOutput, calls=%fused_computation.25 | convolution fusion | flops 2097971200 | bytes 6553604 | tf_op jit(solution)/shard_map/fik,fkj->fij/dot_general | solution.py:43
  226.0 7.5 %all-gather.29.cloned.1.call-done = bf16[1280,1280]{1,0:T(8,128)(2,1)} async-done(((bf16[640,1280]{1,0:T(8,128)(2,1)}), bf16[1280,1280]{1,0:T(8,128)(2,1)}) %all-gather.29.cloned.1.call-update) | async-done | bytes 3276816 | tf_op jit(solution)/shard_map/all_gather | solution.py:31
  233.4 15.6 %all-gather.27.cloned.1.call-done = bf16[1280,1280]{1,0:T(8,128)(2,1)} async-done(((bf16[640,1280]{1,0:T(8,128)(2,1)}), bf16[1280,1280]{1,0:T(8,128)(2,1)}) %all-gather.27.cloned.1.call-update) | async-done | bytes 3276816 | tf_op jit(solution)/shard_map/all_gather | solution.py:32
  249.1 7.3 %fusion.7 = bf16[1280,1280]{1,0:T(8,128)(2,1)S(1)} fusion(bf16[1280,1280]{1,0:T(8,128)(2,1)} %all-gather.27.cloned.1.call-done, bf16[1280,1280]{1,0:T(8,128)(2,1)} %all-gather.29.cloned.1.call-done), kind=kOutput, calls=%fused_computation.11 | convolution fusion | flops 4202496000 | bytes 9830400 | tf_op jit(solution)/shard_map/fik,fkj->fij/dot_general | solution.py:35
  256.4 2.3 fusion.15
  258.7 2.5 copy.11
  261.3 0.6 broadcast.81
  261.9 12.2 %reduce.1 = bf16[640,1280]{1,0:T(8,128)(2,1)} reduce(bf16[640,1,1280]{2,1,0:T(2,128)(2,1)S(1)} %bitcast.46, bf16[]{:T(256)} %broadcast.81), dimensions={1}, to_apply=%bitcast.43.reduce_sub_computation | reduce | bytes 3276802
  274.1 3.9 %reshape.220 = bf16[8,2,51200]{2,1,0:T(2,128)(2,1)} reshape(bf16[640,1280]{1,0:T(8,128)(2,1)} %reduce.1) | data formatting | bytes 3276800
  278.0 5.9 %all-to-all-start.1 = ((bf16[8,2,51200]{2,1,0:T(2,128)(2,1)}), bf16[8,2,51200]{2,1,0:T(2,128)(2,1)}, u32[]{:S(2)}, u32[]{:S(2)}) async-start(bf16[8,2,51200]{2,1,0:T(2,128)(2,1)} %reshape.220), calls=%async_computation.1 | async-start | bytes 3276800 | tf_op jit(solution)/shard_map/all_to_all | solution.py:49
  284.0 3.7 fusion.16
  287.7 2.5 copy.10
  290.3 12.1 %reduce = bf16[640,1280]{1,0:T(8,128)(2,1)} reduce(bf16[640,1,1280]{2,1,0:T(2,128)(2,1)S(1)} %bitcast.47, bf16[]{:T(256)} %broadcast.81), dimensions={1}, to_apply=%bitcast.42.reduce_sub_computation | reduce | bytes 3276802
  302.3 3.7 reshape.222
  306.0 16.8 %all-to-all-done.1 = bf16[8,2,51200]{2,1,0:T(2,128)(2,1)} async-done(((bf16[8,2,51200]{2,1,0:T(2,128)(2,1)}), bf16[8,2,51200]{2,1,0:T(2,128)(2,1)}, u32[]{:S(2)}, u32[]{:S(2)}) %all-to-all-start.1) | async-done | bytes 1638432 | tf_op jit(solution)/shard_map/all_to_all | solution.py:49
  322.8 4.3 %all-to-all-start.2 = ((bf16[8,2,51200]{2,1,0:T(2,128)(2,1)}), bf16[8,2,51200]{2,1,0:T(2,128)(2,1)}, u32[]{:S(2)}, u32[]{:S(2)}) async-start(bf16[8,2,51200]{2,1,0:T(2,128)(2,1)} %reshape.222), calls=%async_computation.2 | async-start | bytes 3276800 | tf_op jit(solution)/shard_map/all_to_all | solution.py:50
  327.1 6.4 %reshape.221 = bf16[640,1,1280]{2,1,0:T(2,128)(2,1)} reshape(bf16[8,2,51200]{2,1,0:T(2,128)(2,1)} %all-to-all-done.1) | data formatting | bytes 3276800
  333.5 2.1 copy.6
  335.6 29.5 %all-to-all-done.2 = bf16[8,2,51200]{2,1,0:T(2,128)(2,1)} async-done(((bf16[8,2,51200]{2,1,0:T(2,128)(2,1)}), bf16[8,2,51200]{2,1,0:T(2,128)(2,1)}, u32[]{:S(2)}, u32[]{:S(2)}) %all-to-all-start.2) | async-done | bytes 1638432 | tf_op jit(solution)/shard_map/all_to_all | solution.py:50
  365.1 6.4 %reshape.223 = bf16[640,1,1280]{2,1,0:T(2,128)(2,1)} reshape(bf16[8,2,51200]{2,1,0:T(2,128)(2,1)} %all-to-all-done.2) | data formatting | bytes 3276800
  371.5 2.1 copy.7
  373.6 3.5 broadcast_divide_fusion
  (33 shorter events, 0.4 us)
Async XLA Ops:
  11.6 89.6 %all-to-all-start = ((f32[8,80,1280]{2,1,0:T(8,128)}), f32[8,80,1280]{2,1,0:T(8,128)S(1)}, u32[]{:S(2)}, u32[]{:S(2)}) async-start(f32[8,80,1280]{2,1,0:T(8,128)} %get-tuple-element.3), calls=%async_computation | async-start | bytes 6553600 | tf_op jit(solution)/shard_map/all_to_all | solution.py:23
  18.9 84.4 %all-gather.15.cloned.1.call-start = ((), (), s32[]{:S(2)}) async-start(), calls=%async_computation.3 | async-start | bytes 4915200 | tf_op jit(solution)/shard_map/all_gather | solution.py:32
  20.5 103.3 %all-gather.17.cloned.1.call-start = ((), (), s32[]{:S(2)}) async-start(), calls=%async_computation.4 | async-start | bytes 4915200 | tf_op jit(solution)/shard_map/all_gather | solution.py:31
  103.2 29.6 %copy-start = (bf16[8,80,1280]{2,1,0:T(8,128)(2,1)S(1)}, bf16[8,80,1280]{2,1,0:T(8,128)(2,1)}, u32[]{:S(2)}) copy-start(bf16[8,80,1280]{2,1,0:T(8,128)(2,1)} %divide_convert_fusion) | copy-start | bytes 4915204
  103.2 46.7 %all-gather.21.cloned.1.call-start = ((), (), s32[]{:S(2)}) async-start(), calls=%async_computation.6 | async-start | bytes 4915200 | tf_op jit(solution)/shard_map/all_gather | solution.py:31
  131.1 1.7 copy-start.5
  136.3 29.1 %all-gather.19.cloned.1.call-start = ((), (), s32[]{:S(2)}) async-start(), calls=%async_computation.5 | async-start | bytes 4915200 | tf_op jit(solution)/shard_map/all_gather | solution.py:32
  142.3 32.2 %copy-start.1 = (bf16[640,1280]{1,0:T(8,128)(2,1)S(1)}, bf16[640,1280]{1,0:T(8,128)(2,1)}, u32[]{:S(2)}) copy-start(bf16[640,1280]{1,0:T(8,128)(2,1)} %convolution_convert_fusion.6) | copy-start | bytes 4915204
  142.3 49.4 %all-gather.25.cloned.1.call-start = ((), (), s32[]{:S(2)}) async-start(), calls=%async_computation.8 | async-start | bytes 4915200 | tf_op jit(solution)/shard_map/all_gather | solution.py:31
  172.8 1.7 copy-start.7
  178.1 29.1 %all-gather.23.cloned.1.call-start = ((), (), s32[]{:S(2)}) async-start(), calls=%async_computation.7 | async-start | bytes 4915200 | tf_op jit(solution)/shard_map/all_gather | solution.py:32
  184.0 32.2 %copy-start.2 = (bf16[640,1280]{1,0:T(8,128)(2,1)S(1)}, bf16[640,1280]{1,0:T(8,128)(2,1)}, u32[]{:S(2)}) copy-start(bf16[640,1280]{1,0:T(8,128)(2,1)} %convolution_convert_fusion.5) | copy-start | bytes 4915204
  184.0 49.4 %all-gather.29.cloned.1.call-start = ((), (), s32[]{:S(2)}) async-start(), calls=%async_computation.10 | async-start | bytes 4915200 | tf_op jit(solution)/shard_map/all_gather | solution.py:31
  214.5 1.7 copy-start.8
  219.8 29.3 %all-gather.27.cloned.1.call-start = ((), (), s32[]{:S(2)}) async-start(), calls=%async_computation.9 | async-start | bytes 4915200 | tf_op jit(solution)/shard_map/all_gather | solution.py:32
  226.0 30.5 %copy-start.3 = (bf16[640,1280]{1,0:T(8,128)(2,1)S(1)}, bf16[640,1280]{1,0:T(8,128)(2,1)}, u32[]{:S(2)}) copy-start(bf16[640,1280]{1,0:T(8,128)(2,1)} %convolution_convert_fusion.3) | copy-start | bytes 4915204
  256.4 2.3 copy-start.6
  274.1 9.9 %copy-start.4 = (bf16[1280,1280]{1,0:T(8,128)(2,1)S(1)}, bf16[1280,1280]{1,0:T(8,128)(2,1)}, u32[]{:S(2)}) copy-start(bf16[1280,1280]{1,0:T(8,128)(2,1)} %all-gather.27.cloned.1.call-done) | copy-start | bytes 9830404
  278.0 44.7 %all-to-all-start.1 = ((bf16[8,2,51200]{2,1,0:T(2,128)(2,1)}), bf16[8,2,51200]{2,1,0:T(2,128)(2,1)}, u32[]{:S(2)}, u32[]{:S(2)}) async-start(bf16[8,2,51200]{2,1,0:T(2,128)(2,1)} %reshape.220), calls=%async_computation.1 | async-start | bytes 3276800 | tf_op jit(solution)/shard_map/all_to_all | solution.py:49
  322.8 42.3 %all-to-all-start.2 = ((bf16[8,2,51200]{2,1,0:T(2,128)(2,1)}), bf16[8,2,51200]{2,1,0:T(2,128)(2,1)}, u32[]{:S(2)}, u32[]{:S(2)}) async-start(bf16[8,2,51200]{2,1,0:T(2,128)(2,1)} %reshape.222), calls=%async_computation.2 | async-start | bytes 3276800 | tf_op jit(solution)/shard_map/all_to_all | solution.py:50
Sparse Core Ops, SparseCore 0:
  21.8 13.7 all-gather.14
  103.3 20.3 all-gather.16
  136.4 13.4 all-gather.20
  151.9 13.4 all-gather.18
  178.2 13.4 all-gather.24
  193.7 13.4 all-gather.22
  219.9 13.4 all-gather.28
  235.5 13.4 all-gather.26
where the time goes:
time: 391 us; the launch traced here: 384 us
  waiting for transfers between devices  136 us (35%)
  blocking collectives  80 us (20%)
  matrix products  63.5 us (16%)
  local copies, waits for them, and re-layouts  36.1 us (9%)
  other arithmetic  35.8 us (9%)
  starting transfers between devices  18.3 us (5%)
  between operations  14.6 us (4%)
    psum x1, blocking collectives, per_device(): lax.psum(jnp.sum(damped * damped, axis=(1, 2)), ('rep', 'blk'))  80 us
    all_gather x4, waiting for transfers between devices, per_device(): lax.all_gather(inverse, 'blk', axis=1, tiled=True)  46.7 us
    all_gather x4, waiting for transfers between devices, per_device(): lax.all_gather(iterate, 'blk', axis=1, tiled=True)  43 us
    unnamed x25, local copies, waits for them, and re-layouts  30.4 us
    all_to_all x1, waiting for transfers between devices, per_device(): lax.all_to_all(inverse, 'rep', split_axis=1, concat_axis=0, tiled=True)  29.5 us
    dot_general x4, matrix products, per_device(): jnp.einsum('fik,fkj->fij', whole_inv, whole_iter, preferred_element_type=...  29.3 us
    unnamed x2, other arithmetic  24.3 us
    dot_general x4, matrix products, per_device(): jnp.einsum('fik,fkj->fij', step_rows, whole_inv, preferred_element_type=j...  21.3 us
  transfers between devices with their start and end apart: 11, of which 9 were waited for; matrix products, arithmetic and copies ran while one was open for 14% of the time, Pallas kernels for 0%

commit v1 on v0

--- a/solution.py
+++ b/solution.py
@@ -19,7 +19,7 @@
     col_ids = lax.iota(jnp.int32, order_full)
     eye_block = (row_ids[:, None] == col_ids[None, :]).astype(jnp.float32)
     damped = factors + damping[:, None, None] * eye_block[None, :, :]
-    factor_norms = jnp.sqrt(lax.psum(jnp.sum(damped * damped, axis=(1, 2)), ("rep", "blk")))
+    factor_norms = jnp.sqrt(lax.psum(lax.psum(jnp.sum(damped * damped, axis=(1, 2)), "blk"), "rep"))
     own_rows = lax.all_to_all(damped, "rep", split_axis=0, concat_axis=1, tiled=True)
     own_norms = lax.dynamic_slice_in_dim(factor_norms, rep_idx * fac_rep, fac_rep)
     iterate = (own_rows / own_norms[:, None, None]).astype(jnp.bfloat16)

time: 391 us -> 383 us (0.980)
  blocking collectives: 80 us -> 67.6 us
  waiting for transfers between devices: 136 us -> 140 us
    psum x1 -> x2, blocking collectives: 80 us -> 67.6 us  [the longest x1 65.1 us: per_device(): lax.psum(lax.psum(jnp.sum(damped * damped, axis=(1, 2)), 'blk'), 'rep')]
  transfers between devices with their start and end apart: 11 -> 11, of which waited for: 9 -> 10; matrix products, arithmetic and copies ran while one was open for 14% -> 14% of each run, Pallas kernels for 0% -> 0%
where the time goes in v1:
time: 383 us; the launch traced here: 375 us
  waiting for transfers between devices  140 us (37%)
  blocking collectives  67.6 us (18%)
  matrix products  63.4 us (17%)
  local copies, waits for them, and re-layouts  36 us (9%)
  other arithmetic  35.5 us (9%)
  starting transfers between devices  18.3 us (5%)
  between operations  14.6 us (4%)
    psum x1, blocking collectives, per_device(): lax.psum(lax.psum(jnp.sum(damped * damped, axis=(1, 2)), 'blk'), 'rep')  65.1 us
    all_gather x4, waiting for transfers between devices, per_device(): lax.all_gather(inverse, 'blk', axis=1, tiled=True)  46.7 us
    all_gather x4, waiting for transfers between devices, per_device(): lax.all_gather(iterate, 'blk', axis=1, tiled=True)  43 us
    unnamed x25, local copies, waits for them, and re-layouts  30.3 us
    all_to_all x1, waiting for transfers between devices, per_device(): lax.all_to_all(inverse, 'rep', split_axis=1, concat_axis=0, tiled=True)  29.5 us
    dot_general x4, matrix products, per_device(): jnp.einsum('fik,fkj->fij', whole_inv, whole_iter, preferred_element_type=...  29.3 us
    unnamed x2, other arithmetic  24 us
    dot_general x4, matrix products, per_device(): jnp.einsum('fik,fkj->fij', step_rows, whole_inv, preferred_element_type=j...  21.3 us
  transfers between devices with their start and end apart: 11, of which 10 were waited for; matrix products, arithmetic and copies ran while one was open for 14% of the time, Pallas kernels for 0%

profile of v1, /device:TPU:0, one launch (start us, length us, event | category | flops | bytes accessed | tf_op | source)
XLA Modules:
  0.0 375.3 jit_solution(17252381644066995238)
XLA Ops:
  7.3 4.3 %multiply_reduce_fusion = (f32[8]{0:T(128)S(1)}, f32[8,80,1280]{2,1,0:T(8,128)}) fusion(f32[8,80,1280]{2,1,0:T(8,128)} %param.2, f32[80,1280]{1,0:T(8,128)S(1)} %fusion.21, f32[8]{0:T(128)} %param.3), kind=kLoop, calls=%fused_computation.20 | loop fusion | flops 3276792 | bytes 6963264 | tf_op jit(solution)/shard_map/reduce_sum | solution.py:22
  11.6 7.3 %all-to-all-start = ((f32[8,80,1280]{2,1,0:T(8,128)}), f32[8,80,1280]{2,1,0:T(8,128)S(1)}, u32[]{:S(2)}, u32[]{:S(2)}) async-start(f32[8,80,1280]{2,1,0:T(8,128)} %get-tuple-element.3), calls=%async_computation | async-start | bytes 6553600 | tf_op jit(solution)/shard_map/all_to_all | solution.py:23
  19.0 1.5 convert_convert_fusion
  20.5 2.5 psum.14
  23.0 65.1 %psum.15 = f32[8]{0:T(128)S(1)} all-reduce(f32[8]{0:T(128)S(1)} %psum.14), channel_id=1, replica_groups=mesh['grp'=2,'rep'=8,'blk'=2] {'rep'}, use_global_device_ids=true, to_apply=%region_2.0 | all-reduce | flops 8 | bytes 64 | tf_op jit(solution)/shard_map/psum | solution.py:22
  88.1 0.7 dynamic_slice.2
  88.8 3.7 all-to-all-done
  92.5 2.1 divide_convert_fusion
  94.7 20.4 %all-gather.17.cloned.1.call-done = bf16[1,1280,1280]{2,1,0:T(8,128)(2,1)} async-done(((bf16[1,640,1280]{2,1,0:T(8,128)(2,1)}), bf16[1,1280,1280]{2,1,0:T(8,128)(2,1)}) %all-gather.17.cloned.1.call-update) | async-done | bytes 3276816 | tf_op jit(solution)/shard_map/all_gather | solution.py:31
  115.1 7.3 %fusion.4 = bf16[1280,1280]{1,0:T(8,128)(2,1)S(1)} fusion(bf16[1,1280,1280]{2,1,0:T(8,128)(2,1)} %all-gather.17.cloned.1.call-done, bf16[1,1280,1280]{2,1,0:T(8,128)(2,1)} %all-gather.15.cloned.1.call-done), kind=kOutput, calls=%fused_computation.8 | convolution fusion | flops 4202496000 | bytes 9830400 | tf_op jit(solution)/shard_map/fik,fkj->fij/dot_general | solution.py:35
  122.5 1.7 copy-done.5
  124.2 3.5 convolution_convert_fusion.6
  127.7 5.9 %fusion.12 = bf16[640,1280]{1,0:T(8,128)(2,1)} fusion(bf16[1,1280,1280]{2,1,0:T(8,128)(2,1)} %all-gather.15.cloned.1.call-done, bf16[1280,1280]{1,0:T(8,128)(2,1)} %copy-done.5, s32[]{:T(128)S(6)} %select_n.10), kind=kOutput, calls=%fused_computation.22 | convolution fusion | flops 2097971200 | bytes 6553604 | tf_op jit(solution)/shard_map/fik,fkj->fij/dot_general | solution.py:43
  133.6 0.2 all-gather.25.cloned.1.call-start
  133.8 7.5 %all-gather.21.cloned.1.call-done = bf16[1280,1280]{1,0:T(8,128)(2,1)} async-done(((bf16[640,1280]{1,0:T(8,128)(2,1)}), bf16[1280,1280]{1,0:T(8,128)(2,1)}) %all-gather.21.cloned.1.call-update) | async-done | bytes 3276816 | tf_op jit(solution)/shard_map/all_gather | solution.py:31
  141.3 15.5 %all-gather.19.cloned.1.call-done = bf16[1280,1280]{1,0:T(8,128)(2,1)} async-done(((bf16[640,1280]{1,0:T(8,128)(2,1)}), bf16[1280,1280]{1,0:T(8,128)(2,1)}) %all-gather.19.cloned.1.call-update) | async-done | bytes 3276816 | tf_op jit(solution)/shard_map/all_gather | solution.py:32
  156.8 7.3 %fusion.5 = bf16[1280,1280]{1,0:T(8,128)(2,1)S(1)} fusion(bf16[1280,1280]{1,0:T(8,128)(2,1)} %all-gather.19.cloned.1.call-done, bf16[1280,1280]{1,0:T(8,128)(2,1)} %all-gather.21.cloned.1.call-done), kind=kOutput, calls=%fused_computation.9 | convolution fusion | flops 4202496000 | bytes 9830400 | tf_op jit(solution)/shard_map/fik,fkj->fij/dot_general | solution.py:35
  164.2 1.7 copy-done.7
  165.9 3.5 convolution_convert_fusion.5
  169.4 5.9 %convolution_convert_fusion.4 = bf16[640,1280]{1,0:T(8,128)(2,1)} fusion(bf16[1280,1280]{1,0:T(8,128)(2,1)} %all-gather.19.cloned.1.call-done, bf16[1280,1280]{1,0:T(8,128)(2,1)} %copy-done.7, s32[]{:T(128)S(6)} %select_n.10), kind=kOutput, calls=%fused_computation.27 | convolution fusion | flops 2097971200 | bytes 6553604 | tf_op jit(solution)/shard_map/fik,fkj->fij/dot_general | solution.py:43
  175.4 7.6 %all-gather.25.cloned.1.call-done = bf16[1280,1280]{1,0:T(8,128)(2,1)} async-done(((bf16[640,1280]{1,0:T(8,128)(2,1)}), bf16[1280,1280]{1,0:T(8,128)(2,1)}) %all-gather.25.cloned.1.call-update) | async-done | bytes 3276816 | tf_op jit(solution)/shard_map/all_gather | solution.py:31
  183.0 15.5 %all-gather.23.cloned.1.call-done = bf16[1280,1280]{1,0:T(8,128)(2,1)} async-done(((bf16[640,1280]{1,0:T(8,128)(2,1)}), bf16[1280,1280]{1,0:T(8,128)(2,1)}) %all-gather.23.cloned.1.call-update) | async-done | bytes 3276816 | tf_op jit(solution)/shard_map/all_gather | solution.py:32
  198.5 7.3 %fusion.6 = bf16[1280,1280]{1,0:T(8,128)(2,1)S(1)} fusion(bf16[1280,1280]{1,0:T(8,128)(2,1)} %all-gather.23.cloned.1.call-done, bf16[1280,1280]{1,0:T(8,128)(2,1)} %all-gather.25.cloned.1.call-done), kind=kOutput, calls=%fused_computation.10 | convolution fusion | flops 4202496000 | bytes 9830400 | tf_op jit(solution)/shard_map/fik,fkj->fij/dot_general | solution.py:35
  205.9 1.7 copy-done.8
  207.6 3.5 convolution_convert_fusion.3
  211.1 0.3 all-gather.27.cloned.1.call-start
  211.3 5.9 %convolution_convert_fusion.2 = bf16[640,1280]{1,0:T(8,128)(2,1)} fusion(bf16[1280,1280]{1,0:T(8,128)(2,1)} %all-gather.23.cloned.1.call-done, bf16[1280,1280]{1,0:T(8,128)(2,1)} %copy-done.8, s32[]{:T(128)S(6)} %select_n.10), kind=kOutput, calls=%fused_computation.25 | convolution fusion | flops 2097971200 | bytes 6553604 | tf_op jit(solution)/shard_map/fik,fkj->fij/dot_general | solution.py:43
  217.3 7.5 %all-gather.29.cloned.1.call-done = bf16[1280,1280]{1,0:T(8,128)(2,1)} async-done(((bf16[640,1280]{1,0:T(8,128)(2,1)}), bf16[1280,1280]{1,0:T(8,128)(2,1)}) %all-gather.29.cloned.1.call-update) | async-done | bytes 3276816 | tf_op jit(solution)/shard_map/all_gather | solution.py:31
  224.7 15.6 %all-gather.27.cloned.1.call-done = bf16[1280,1280]{1,0:T(8,128)(2,1)} async-done(((bf16[640,1280]{1,0:T(8,128)(2,1)}), bf16[1280,1280]{1,0:T(8,128)(2,1)}) %all-gather.27.cloned.1.call-update) | async-done | bytes 3276816 | tf_op jit(solution)/shard_map/all_gather | solution.py:32
  240.4 7.3 %fusion.7 = bf16[1280,1280]{1,0:T(8,128)(2,1)S(1)} fusion(bf16[1280,1280]{1,0:T(8,128)(2,1)} %all-gather.27.cloned.1.call-done, bf16[1280,1280]{1,0:T(8,128)(2,1)} %all-gather.29.cloned.1.call-done), kind=kOutput, calls=%fused_computation.11 | convolution fusion | flops 4202496000 | bytes 9830400 | tf_op jit(solution)/shard_map/fik,fkj->fij/dot_general | solution.py:35
  247.7 2.3 fusion.15
  250.0 2.5 copy.11
  252.6 0.5 broadcast.81
  253.1 12.1 %reduce.1 = bf16[640,1280]{1,0:T(8,128)(2,1)} reduce(bf16[640,1,1280]{2,1,0:T(2,128)(2,1)S(1)} %bitcast.46, bf16[]{:T(256)} %broadcast.81), dimensions={1}, to_apply=%bitcast.43.reduce_sub_computation | reduce | bytes 3276802
  265.2 3.9 %reshape.220 = bf16[8,2,51200]{2,1,0:T(2,128)(2,1)} reshape(bf16[640,1280]{1,0:T(8,128)(2,1)} %reduce.1) | data formatting | bytes 3276800
  269.1 5.9 %all-to-all-start.1 = ((bf16[8,2,51200]{2,1,0:T(2,128)(2,1)}), bf16[8,2,51200]{2,1,0:T(2,128)(2,1)}, u32[]{:S(2)}, u32[]{:S(2)}) async-start(bf16[8,2,51200]{2,1,0:T(2,128)(2,1)} %reshape.220), calls=%async_computation.1 | async-start | bytes 3276800 | tf_op jit(solution)/shard_map/all_to_all | solution.py:49
  275.0 3.7 fusion.16
  278.7 2.5 copy.10
  281.3 11.9 %reduce = bf16[640,1280]{1,0:T(8,128)(2,1)} reduce(bf16[640,1,1280]{2,1,0:T(2,128)(2,1)S(1)} %bitcast.47, bf16[]{:T(256)} %broadcast.81), dimensions={1}, to_apply=%bitcast.42.reduce_sub_computation | reduce | bytes 3276802
  293.2 3.7 reshape.222
  296.9 16.9 %all-to-all-done.1 = bf16[8,2,51200]{2,1,0:T(2,128)(2,1)} async-done(((bf16[8,2,51200]{2,1,0:T(2,128)(2,1)}), bf16[8,2,51200]{2,1,0:T(2,128)(2,1)}, u32[]{:S(2)}, u32[]{:S(2)}) %all-to-all-start.1) | async-done | bytes 1638432 | tf_op jit(solution)/shard_map/all_to_all | solution.py:49
  313.8 4.3 %all-to-all-start.2 = ((bf16[8,2,51200]{2,1,0:T(2,128)(2,1)}), bf16[8,2,51200]{2,1,0:T(2,128)(2,1)}, u32[]{:S(2)}, u32[]{:S(2)}) async-start(bf16[8,2,51200]{2,1,0:T(2,128)(2,1)} %reshape.222), calls=%async_computation.2 | async-start | bytes 3276800 | tf_op jit(solution)/shard_map/all_to_all | solution.py:50
  318.1 6.4 %reshape.221 = bf16[640,1,1280]{2,1,0:T(2,128)(2,1)} reshape(bf16[8,2,51200]{2,1,0:T(2,128)(2,1)} %all-to-all-done.1) | data formatting | bytes 3276800
  324.5 2.1 copy.6
  326.6 29.5 %all-to-all-done.2 = bf16[8,2,51200]{2,1,0:T(2,128)(2,1)} async-done(((bf16[8,2,51200]{2,1,0:T(2,128)(2,1)}), bf16[8,2,51200]{2,1,0:T(2,128)(2,1)}, u32[]{:S(2)}, u32[]{:S(2)}) %all-to-all-start.2) | async-done | bytes 1638432 | tf_op jit(solution)/shard_map/all_to_all | solution.py:50
  356.2 6.4 %reshape.223 = bf16[640,1,1280]{2,1,0:T(2,128)(2,1)} reshape(bf16[8,2,51200]{2,1,0:T(2,128)(2,1)} %all-to-all-done.2) | data formatting | bytes 3276800
  362.5 2.1 copy.7
  364.7 3.5 broadcast_divide_fusion
  (34 shorter events, 0.5 us)
Async XLA Ops:
  11.6 80.9 %all-to-all-start = ((f32[8,80,1280]{2,1,0:T(8,128)}), f32[8,80,1280]{2,1,0:T(8,128)S(1)}, u32[]{:S(2)}, u32[]{:S(2)}) async-start(f32[8,80,1280]{2,1,0:T(8,128)} %get-tuple-element.3), calls=%async_computation | async-start | bytes 6553600 | tf_op jit(solution)/shard_map/all_to_all | solution.py:23
  18.9 75.8 %all-gather.15.cloned.1.call-start = ((), (), s32[]{:S(2)}) async-start(), calls=%async_computation.3 | async-start | bytes 4915200 | tf_op jit(solution)/shard_map/all_gather | solution.py:32
  20.5 94.6 %all-gather.17.cloned.1.call-start = ((), (), s32[]{:S(2)}) async-start(), calls=%async_computation.4 | async-start | bytes 4915200 | tf_op jit(solution)/shard_map/all_gather | solution.py:31
  94.6 29.6 %copy-start = (bf16[8,80,1280]{2,1,0:T(8,128)(2,1)S(1)}, bf16[8,80,1280]{2,1,0:T(8,128)(2,1)}, u32[]{:S(2)}) copy-start(bf16[8,80,1280]{2,1,0:T(8,128)(2,1)} %divide_convert_fusion) | copy-start | bytes 4915204
  94.6 46.7 %all-gather.21.cloned.1.call-start = ((), (), s32[]{:S(2)}) async-start(), calls=%async_computation.6 | async-start | bytes 4915200 | tf_op jit(solution)/shard_map/all_gather | solution.py:31
  122.4 1.7 copy-start.5
  127.7 29.1 %all-gather.19.cloned.1.call-start = ((), (), s32[]{:S(2)}) async-start(), calls=%async_computation.5 | async-start | bytes 4915200 | tf_op jit(solution)/shard_map/all_gather | solution.py:32
  133.6 32.2 %copy-start.1 = (bf16[640,1280]{1,0:T(8,128)(2,1)S(1)}, bf16[640,1280]{1,0:T(8,128)(2,1)}, u32[]{:S(2)}) copy-start(bf16[640,1280]{1,0:T(8,128)(2,1)} %convolution_convert_fusion.6) | copy-start | bytes 4915204
  133.6 49.4 %all-gather.25.cloned.1.call-start = ((), (), s32[]{:S(2)}) async-start(), calls=%async_computation.8 | async-start | bytes 4915200 | tf_op jit(solution)/shard_map/all_gather | solution.py:31
  164.1 1.7 copy-start.7
  169.4 29.1 %all-gather.23.cloned.1.call-start = ((), (), s32[]{:S(2)}) async-start(), calls=%async_computation.7 | async-start | bytes 4915200 | tf_op jit(solution)/shard_map/all_gather | solution.py:32
  175.3 32.2 %copy-start.2 = (bf16[640,1280]{1,0:T(8,128)(2,1)S(1)}, bf16[640,1280]{1,0:T(8,128)(2,1)}, u32[]{:S(2)}) copy-start(bf16[640,1280]{1,0:T(8,128)(2,1)} %convolution_convert_fusion.5) | copy-start | bytes 4915204
  175.3 49.4 %all-gather.29.cloned.1.call-start = ((), (), s32[]{:S(2)}) async-start(), calls=%async_computation.10 | async-start | bytes 4915200 | tf_op jit(solution)/shard_map/all_gather | solution.py:31
  205.9 1.7 copy-start.8
  211.1 29.3 %all-gather.27.cloned.1.call-start = ((), (), s32[]{:S(2)}) async-start(), calls=%async_computation.9 | async-start | bytes 4915200 | tf_op jit(solution)/shard_map/all_gather | solution.py:32
  217.2 30.5 %copy-start.3 = (bf16[640,1280]{1,0:T(8,128)(2,1)S(1)}, bf16[640,1280]{1,0:T(8,128)(2,1)}, u32[]{:S(2)}) copy-start(bf16[640,1280]{1,0:T(8,128)(2,1)} %convolution_convert_fusion.3) | copy-start | bytes 4915204
  247.7 2.3 copy-start.6
  265.2 9.8 %copy-start.4 = (bf16[1280,1280]{1,0:T(8,128)(2,1)S(1)}, bf16[1280,1280]{1,0:T(8,128)(2,1)}, u32[]{:S(2)}) copy-start(bf16[1280,1280]{1,0:T(8,128)(2,1)} %all-gather.27.cloned.1.call-done) | copy-start | bytes 9830404
  269.1 44.8 %all-to-all-start.1 = ((bf16[8,2,51200]{2,1,0:T(2,128)(2,1)}), bf16[8,2,51200]{2,1,0:T(2,128)(2,1)}, u32[]{:S(2)}, u32[]{:S(2)}) async-start(bf16[8,2,51200]{2,1,0:T(2,128)(2,1)} %reshape.220), calls=%async_computation.1 | async-start | bytes 3276800 | tf_op jit(solution)/shard_map/all_to_all | solution.py:49
  313.8 42.3 %all-to-all-start.2 = ((bf16[8,2,51200]{2,1,0:T(2,128)(2,1)}), bf16[8,2,51200]{2,1,0:T(2,128)(2,1)}, u32[]{:S(2)}, u32[]{:S(2)}) async-start(bf16[8,2,51200]{2,1,0:T(2,128)(2,1)} %reshape.222), calls=%async_computation.2 | async-start | bytes 3276800 | tf_op jit(solution)/shard_map/all_to_all | solution.py:50
Sparse Core Ops, SparseCore 0:
  21.8 13.7 all-gather.14
  94.7 20.3 all-gather.16
  127.8 13.4 all-gather.20
  143.3 13.4 all-gather.18
  169.5 13.4 all-gather.24
  185.0 13.4 all-gather.22
  211.2 13.4 all-gather.28
  226.8 13.4 all-gather.26
